TPU v7x, 32 devices: a whole 2x2x4 slice. The times are simulated.
32 devices in a mesh: vec: 4 (over z), field: 4 (over x, core), rep: 2 (over y).
Axes of the slice: x: 2, y: 2, z: 4, core: 2. Of those that a mesh axis runs over, the one named last changes fastest.
Arguments:
- dosage: bfloat16 [96, 65536], P('vec', 'field'), may hold values from 0 to 2
Outputs:
- ccc: float32 [2, 96, 2, 24, 2, 96], P('rep', ('vec', 'field'))
All inputs are finite; a program needn't handle non-finite values.
Results may differ from a plain program's by a relative error of at most 0.0003.
Values may be sent and summed in bfloat16 or wider, within the bound.
A program may use at most 64 MiB of HBM per device.

v0:
```python
import jax
import jax.numpy as jnp
from jax import lax
from jax.sharding import PartitionSpec as P

F = 65536
S = 2


def passed_along(value, axis, by):
    count = lax.axis_size(axis)
    return lax.ppermute(value, axis, [(i, (i + by) % count) for i in range(count)])


def contract(first_rows, third_rows, partner_rows):
    field_width = first_rows.shape[1]
    block_width = min(1024, field_width)
    block_count = field_width // block_width

    def add_block(block_id, running):
        offset = block_id * block_width
        first_cut = lax.dynamic_slice_in_dim(first_rows, offset, block_width, 1)
        third_cut = lax.dynamic_slice_in_dim(third_rows, offset, block_width, 1)
        partner_cut = lax.dynamic_slice_in_dim(partner_rows, offset, block_width, 1)
        pair_rows = (first_cut[:, None, :] * third_cut[None, :, :]).reshape(-1, block_width)
        return running + lax.dot_general(
            pair_rows, partner_cut, (((1,), (1,)), ((), ())), preferred_element_type=jnp.float32
        )

    start_value = jnp.zeros(
        (first_rows.shape[0] * third_rows.shape[0], partner_rows.shape[0]), jnp.float32
    )
    return lax.fori_loop(0, block_count, add_block, start_value)


def row_totals(rows):
    return jnp.sum(rows.astype(jnp.float32), axis=1)


def body(dosage):
    vectors = dosage.shape[0]
    field_place = lax.axis_index("field")
    share_rows = vectors // lax.axis_size("field")
    rep_plane = lax.axis_index("rep")
    other_count = (2.0 - dosage.astype(jnp.float32)).astype(jnp.bfloat16)
    stacked = jnp.stack([other_count, dosage], axis=1)
    vector_rows = stacked.reshape(2 * vectors, dosage.shape[1])
    third_near = passed_along(vector_rows, "vec", 1)
    third_far = passed_along(third_near, "vec", 1)
    third_rows = jnp.where(rep_plane == 0, third_near, third_far)
    partners = []
    current = vector_rows
    for hop_count in range(S):
        current = passed_along(current, "vec", -1)
        partners.append(current)
    partner_rows = jnp.concatenate(partners, axis=0)
    own_total, third_total, partner_total = lax.psum(
        (row_totals(vector_rows), row_totals(third_rows), row_totals(partner_rows)), "field"
    )
    gain_own = (1.0 - own_total / (3.0 * F)).reshape(vectors, 2)
    gain_third = (1.0 - third_total / (3.0 * F)).reshape(vectors, 2)
    gain_partner = 1.0 - partner_total / (3.0 * F)
    tables = contract(vector_rows, third_rows, partner_rows)
    tables = tables.reshape(vectors, 2, vectors, 2, tables.shape[1])
    summed = lax.psum_scatter(tables, "field", scatter_dimension=0, tiled=True)
    gain_first = lax.dynamic_slice_in_dim(gain_own, field_place * share_rows, share_rows, 0)
    result = (
        4.5
        / (8.0 * F)
        * summed
        * gain_first[:, :, None, None, None]
        * gain_third[None, None, :, :, None]
        * gain_partner
    )
    return result[None]


def solution(mesh):
    placed = (P("vec", "field"),)
    return jax.shard_map(
        body,
        mesh=mesh,
        in_specs=placed,
        out_specs=P("rep", ("vec", "field"), None, None, None, None),
        check_vma=False,
    )
```

profile of v0, /device:TPU:0, one launch (start us, length us, event | category | flops | bytes accessed | tf_op | source)
XLA Modules:
  0.0 256.0 jit_solution(1144768919272300027)
XLA Ops:
  6.5 1.3 fusion.2
  7.9 0.9 copy-done.3
  9.0 1.6 copy.10
  11.2 5.1 %collective-permute-start.2 = (bf16[48,16384]{1,0:T(8,128)(2,1)S(1)}, bf16[48,16384]{1,0:T(8,128)(2,1)}, u32[]{:S(2)}, u32[]{:S(2)}) collective-permute-start(bf16[48,16384]{1,0:T(8,128)(2,1)S(1)} %reshape.25), channel_id=1, source_target_pairs={{0,24},{8,0},{16,8},{24,16},{1,25},{9,1},{17,9},{25,17},{2,26},{10... | collective-permute-start | bytes 4718600 | tf_op jit(solution)/shard_map/ppermute | solution.py:12
  16.4 34.8 %collective-permute-done.2 = bf16[48,16384]{1,0:T(8,128)(2,1)} collective-permute-done((bf16[48,16384]{1,0:T(8,128)(2,1)S(1)}, bf16[48,16384]{1,0:T(8,128)(2,1)}, u32[]{:S(2)}, u32[]{:S(2)}) %collective-permute-start.2) | collective-permute-done | bytes 1572896 | tf_op jit(solution)/shard_map/ppermute | solution.py:12
  51.2 4.4 %collective-permute-start.3 = (bf16[48,16384]{1,0:T(8,128)(2,1)}, bf16[48,16384]{1,0:T(8,128)(2,1)S(1)}, u32[]{:S(2)}, u32[]{:S(2)}) collective-permute-start(bf16[48,16384]{1,0:T(8,128)(2,1)} %collective-permute-done.2), channel_id=1, source_target_pairs={{0,24},{8,0},{16,8},{24,16},{1,25},{9,1},{17,9},{25,17},{2,26},{10... | collective-permute-start | bytes 4718600 | tf_op jit(solution)/shard_map/ppermute | solution.py:12
  55.6 30.4 %collective-permute-done = bf16[48,16384]{1,0:T(8,128)(2,1)} collective-permute-done((bf16[48,16384]{1,0:T(8,128)(2,1)S(1)}, bf16[48,16384]{1,0:T(8,128)(2,1)}, u32[]{:S(2)}, u32[]{:S(2)}) %collective-permute-start) | collective-permute-done | bytes 1572896 | tf_op jit(solution)/shard_map/ppermute | solution.py:12
  85.9 1.5 collective-permute-start.1
  87.5 1.5 constant_dynamic-update-slice_fusion.1
  89.0 63.1 %collective-permute-done.1 = bf16[48,16384]{1,0:T(8,128)(2,1)S(1)} collective-permute-done((bf16[48,16384]{1,0:T(8,128)(2,1)}, bf16[48,16384]{1,0:T(8,128)(2,1)S(1)}, u32[]{:S(2)}, u32[]{:S(2)}) %collective-permute-start.1) | collective-permute-done | bytes 1572896 | tf_op jit(solution)/shard_map/ppermute | solution.py:12
  152.1 2.1 convert_reduce_fusion.1
  154.3 1.6 copy-done
  155.9 62.1 %while.14 = (s32[]{:T(128)}, f32[2304,96]{0,1:T(8,128)S(1)}, bf16[48,16384]{1,0:T(8,128)(2,1)}, bf16[48,16384]{1,0:T(8,128)(2,1)S(1)}, bf16[96,16384]{1,0:T(8,12...) while((s32[]{:T(128)}, f32[2304,96]{0,1:T(8,128)S(1)}, bf16[48,16384]{1,0:T(8,128)(2,1)}, ...), condition=%wide.region_1.2_spmd.clone, body=%wide.region_0.1_spmd.clone.sunk | while | flops 455786496 | bytes 11993253 | solution.py:33
  157.2 2.6 %convolution_add_fusion.2 = f32[2304,96]{0,1:T(8,128)S(1)} fusion(bf16[2304,1024]{1,0:T(8,128)(2,1)S(1)} %bitcast.12, f32[2304,96]{0,1:T(8,128)S(1)} %get-tuple-element.182, pred[]{:T(512)S(6)} %compare.3, bf16[96,16384]{1,0:T(8,128)(2,1)} %get-tuple-element.194, s32[]{:T(128)S(6)} %select_n.29), kind=kOutput, calls=%fused_computation.clone.1 | convolution fusion | flops 453427200 | bytes 6684677 | tf_op jit(solution)/shard_map/while/body/eval_jaxpr/dot_general | solution.py:26
  159.8 0.9 constant_dynamic-slice_fusion.3
  161.1 2.6 %convolution_add_fusion.2 = f32[2304,96]{0,1:T(8,128)S(1)} fusion(bf16[2304,1024]{1,0:T(8,128)(2,1)S(1)} %bitcast.12, f32[2304,96]{0,1:T(8,128)S(1)} %get-tuple-element.182, pred[]{:T(512)S(6)} %compare.3, bf16[96,16384]{1,0:T(8,128)(2,1)} %get-tuple-element.194, s32[]{:T(128)S(6)} %select_n.29), kind=kOutput, calls=%fused_computation.clone.1 | convolution fusion | flops 453427200 | bytes 6684677 | tf_op jit(solution)/shard_map/while/body/eval_jaxpr/dot_general | solution.py:26
  163.7 0.9 constant_dynamic-slice_fusion.3
  164.9 2.6 %convolution_add_fusion.2 = f32[2304,96]{0,1:T(8,128)S(1)} fusion(bf16[2304,1024]{1,0:T(8,128)(2,1)S(1)} %bitcast.12, f32[2304,96]{0,1:T(8,128)S(1)} %get-tuple-element.182, pred[]{:T(512)S(6)} %compare.3, bf16[96,16384]{1,0:T(8,128)(2,1)} %get-tuple-element.194, s32[]{:T(128)S(6)} %select_n.29), kind=kOutput, calls=%fused_computation.clone.1 | convolution fusion | flops 453427200 | bytes 6684677 | tf_op jit(solution)/shard_map/while/body/eval_jaxpr/dot_general | solution.py:26
  167.6 0.9 constant_dynamic-slice_fusion.3
  168.8 2.6 %convolution_add_fusion.2 = f32[2304,96]{0,1:T(8,128)S(1)} fusion(bf16[2304,1024]{1,0:T(8,128)(2,1)S(1)} %bitcast.12, f32[2304,96]{0,1:T(8,128)S(1)} %get-tuple-element.182, pred[]{:T(512)S(6)} %compare.3, bf16[96,16384]{1,0:T(8,128)(2,1)} %get-tuple-element.194, s32[]{:T(128)S(6)} %select_n.29), kind=kOutput, calls=%fused_computation.clone.1 | convolution fusion | flops 453427200 | bytes 6684677 | tf_op jit(solution)/shard_map/while/body/eval_jaxpr/dot_general | solution.py:26
  171.5 0.9 constant_dynamic-slice_fusion.3
  172.7 2.6 %convolution_add_fusion.2 = f32[2304,96]{0,1:T(8,128)S(1)} fusion(bf16[2304,1024]{1,0:T(8,128)(2,1)S(1)} %bitcast.12, f32[2304,96]{0,1:T(8,128)S(1)} %get-tuple-element.182, pred[]{:T(512)S(6)} %compare.3, bf16[96,16384]{1,0:T(8,128)(2,1)} %get-tuple-element.194, s32[]{:T(128)S(6)} %select_n.29), kind=kOutput, calls=%fused_computation.clone.1 | convolution fusion | flops 453427200 | bytes 6684677 | tf_op jit(solution)/shard_map/while/body/eval_jaxpr/dot_general | solution.py:26
  175.3 0.9 constant_dynamic-slice_fusion.3
  176.6 2.6 %convolution_add_fusion.2 = f32[2304,96]{0,1:T(8,128)S(1)} fusion(bf16[2304,1024]{1,0:T(8,128)(2,1)S(1)} %bitcast.12, f32[2304,96]{0,1:T(8,128)S(1)} %get-tuple-element.182, pred[]{:T(512)S(6)} %compare.3, bf16[96,16384]{1,0:T(8,128)(2,1)} %get-tuple-element.194, s32[]{:T(128)S(6)} %select_n.29), kind=kOutput, calls=%fused_computation.clone.1 | convolution fusion | flops 453427200 | bytes 6684677 | tf_op jit(solution)/shard_map/while/body/eval_jaxpr/dot_general | solution.py:26
  179.2 0.9 constant_dynamic-slice_fusion.3
  180.5 2.6 %convolution_add_fusion.2 = f32[2304,96]{0,1:T(8,128)S(1)} fusion(bf16[2304,1024]{1,0:T(8,128)(2,1)S(1)} %bitcast.12, f32[2304,96]{0,1:T(8,128)S(1)} %get-tuple-element.182, pred[]{:T(512)S(6)} %compare.3, bf16[96,16384]{1,0:T(8,128)(2,1)} %get-tuple-element.194, s32[]{:T(128)S(6)} %select_n.29), kind=kOutput, calls=%fused_computation.clone.1 | convolution fusion | flops 453427200 | bytes 6684677 | tf_op jit(solution)/shard_map/while/body/eval_jaxpr/dot_general | solution.py:26
  183.1 0.9 constant_dynamic-slice_fusion.3
  184.3 2.6 %convolution_add_fusion.2 = f32[2304,96]{0,1:T(8,128)S(1)} fusion(bf16[2304,1024]{1,0:T(8,128)(2,1)S(1)} %bitcast.12, f32[2304,96]{0,1:T(8,128)S(1)} %get-tuple-element.182, pred[]{:T(512)S(6)} %compare.3, bf16[96,16384]{1,0:T(8,128)(2,1)} %get-tuple-element.194, s32[]{:T(128)S(6)} %select_n.29), kind=kOutput, calls=%fused_computation.clone.1 | convolution fusion | flops 453427200 | bytes 6684677 | tf_op jit(solution)/shard_map/while/body/eval_jaxpr/dot_general | solution.py:26
  187.0 0.9 constant_dynamic-slice_fusion.3
  188.2 2.6 %convolution_add_fusion.2 = f32[2304,96]{0,1:T(8,128)S(1)} fusion(bf16[2304,1024]{1,0:T(8,128)(2,1)S(1)} %bitcast.12, f32[2304,96]{0,1:T(8,128)S(1)} %get-tuple-element.182, pred[]{:T(512)S(6)} %compare.3, bf16[96,16384]{1,0:T(8,128)(2,1)} %get-tuple-element.194, s32[]{:T(128)S(6)} %select_n.29), kind=kOutput, calls=%fused_computation.clone.1 | convolution fusion | flops 453427200 | bytes 6684677 | tf_op jit(solution)/shard_map/while/body/eval_jaxpr/dot_general | solution.py:26
  190.9 0.9 constant_dynamic-slice_fusion.3
  192.1 2.6 %convolution_add_fusion.2 = f32[2304,96]{0,1:T(8,128)S(1)} fusion(bf16[2304,1024]{1,0:T(8,128)(2,1)S(1)} %bitcast.12, f32[2304,96]{0,1:T(8,128)S(1)} %get-tuple-element.182, pred[]{:T(512)S(6)} %compare.3, bf16[96,16384]{1,0:T(8,128)(2,1)} %get-tuple-element.194, s32[]{:T(128)S(6)} %select_n.29), kind=kOutput, calls=%fused_computation.clone.1 | convolution fusion | flops 453427200 | bytes 6684677 | tf_op jit(solution)/shard_map/while/body/eval_jaxpr/dot_general | solution.py:26
  194.8 0.9 constant_dynamic-slice_fusion.3
  196.0 2.6 %convolution_add_fusion.2 = f32[2304,96]{0,1:T(8,128)S(1)} fusion(bf16[2304,1024]{1,0:T(8,128)(2,1)S(1)} %bitcast.12, f32[2304,96]{0,1:T(8,128)S(1)} %get-tuple-element.182, pred[]{:T(512)S(6)} %compare.3, bf16[96,16384]{1,0:T(8,128)(2,1)} %get-tuple-element.194, s32[]{:T(128)S(6)} %select_n.29), kind=kOutput, calls=%fused_computation.clone.1 | convolution fusion | flops 453427200 | bytes 6684677 | tf_op jit(solution)/shard_map/while/body/eval_jaxpr/dot_general | solution.py:26
  198.6 0.9 constant_dynamic-slice_fusion.3
  199.9 2.6 %convolution_add_fusion.2 = f32[2304,96]{0,1:T(8,128)S(1)} fusion(bf16[2304,1024]{1,0:T(8,128)(2,1)S(1)} %bitcast.12, f32[2304,96]{0,1:T(8,128)S(1)} %get-tuple-element.182, pred[]{:T(512)S(6)} %compare.3, bf16[96,16384]{1,0:T(8,128)(2,1)} %get-tuple-element.194, s32[]{:T(128)S(6)} %select_n.29), kind=kOutput, calls=%fused_computation.clone.1 | convolution fusion | flops 453427200 | bytes 6684677 | tf_op jit(solution)/shard_map/while/body/eval_jaxpr/dot_general | solution.py:26
  202.5 0.9 constant_dynamic-slice_fusion.3
  203.8 2.6 %convolution_add_fusion.2 = f32[2304,96]{0,1:T(8,128)S(1)} fusion(bf16[2304,1024]{1,0:T(8,128)(2,1)S(1)} %bitcast.12, f32[2304,96]{0,1:T(8,128)S(1)} %get-tuple-element.182, pred[]{:T(512)S(6)} %compare.3, bf16[96,16384]{1,0:T(8,128)(2,1)} %get-tuple-element.194, s32[]{:T(128)S(6)} %select_n.29), kind=kOutput, calls=%fused_computation.clone.1 | convolution fusion | flops 453427200 | bytes 6684677 | tf_op jit(solution)/shard_map/while/body/eval_jaxpr/dot_general | solution.py:26
  207.6 2.6 %convolution_add_fusion.2 = f32[2304,96]{0,1:T(8,128)S(1)} fusion(bf16[2304,1024]{1,0:T(8,128)(2,1)S(1)} %bitcast.12, f32[2304,96]{0,1:T(8,128)S(1)} %get-tuple-element.182, pred[]{:T(512)S(6)} %compare.3, bf16[96,16384]{1,0:T(8,128)(2,1)} %get-tuple-element.194, s32[]{:T(128)S(6)} %select_n.29), kind=kOutput, calls=%fused_computation.clone.1 | convolution fusion | flops 453427200 | bytes 6684677 | tf_op jit(solution)/shard_map/while/body/eval_jaxpr/dot_general | solution.py:26
  210.3 0.9 constant_dynamic-slice_fusion.3
  211.5 2.6 %convolution_add_fusion.2 = f32[2304,96]{0,1:T(8,128)S(1)} fusion(bf16[2304,1024]{1,0:T(8,128)(2,1)S(1)} %bitcast.12, f32[2304,96]{0,1:T(8,128)S(1)} %get-tuple-element.182, pred[]{:T(512)S(6)} %compare.3, bf16[96,16384]{1,0:T(8,128)(2,1)} %get-tuple-element.194, s32[]{:T(128)S(6)} %select_n.29), kind=kOutput, calls=%fused_computation.clone.1 | convolution fusion | flops 453427200 | bytes 6684677 | tf_op jit(solution)/shard_map/while/body/eval_jaxpr/dot_general | solution.py:26
  215.4 2.6 %convolution_add_fusion.2 = f32[2304,96]{0,1:T(8,128)S(1)} fusion(bf16[2304,1024]{1,0:T(8,128)(2,1)S(1)} %bitcast.12, f32[2304,96]{0,1:T(8,128)S(1)} %get-tuple-element.182, pred[]{:T(512)S(6)} %compare.3, bf16[96,16384]{1,0:T(8,128)(2,1)} %get-tuple-element.194, s32[]{:T(128)S(6)} %select_n.29), kind=kOutput, calls=%fused_computation.clone.1 | convolution fusion | flops 453427200 | bytes 6684677 | tf_op jit(solution)/shard_map/while/body/eval_jaxpr/dot_general | solution.py:26
  218.0 1.4 copy.11
  219.4 2.5 copy.12
  222.0 1.7 convert_reduce_fusion.2
  224.4 5.7 %all-reduce = (f32[96]{0:T(128)S(1)}, f32[48]{0:T(128)S(1)}, f32[48]{0:T(128)S(1)}) all-reduce(f32[96]{0:T(128)S(1)} %convert_reduce_fusion, f32[48]{0:T(128)S(1)} %get-tuple-element.131, f32[48]{0:T(128)S(1)} %reduce_sum.30), channel_id=1, replica_groups=mesh['vec'=4,'field'=4,'rep'=2] {'field'}, use_global_device_ids=true, to_apply=%region_8.9 | all-reduce | flops 192 | bytes 1536 | tf_op jit(solution)/shard_map/psum | solution.py:57
  230.5 16.8 %reduce-scatter.2.cloned.1.call-done = f32[6,2,24,2,96]{4,2,3,1,0:T(8,128)} async-done(((f32[24,2,24,2,96]{4,2,3,1,0:T(8,128)}), f32[6,2,24,2,96]{4,2,3,1,0:T(8,128)}) %reduce-scatter.2.cloned.1.call-update) | async-done | bytes 221200 | tf_op jit(solution)/shard_map/reduce_scatter | solution.py:65
  247.2 1.1 multiply_bitcast_fusion
  (45 shorter events, 10.5 us)
Async XLA Ops:
  6.5 2.3 copy-start.2
  6.5 240.7 %reduce-scatter.2.cloned.1.call-start = ((), (), s32[]{:S(2)}) async-start(), calls=%async_computation.1 | async-start | bytes 1474560 | tf_op jit(solution)/shard_map/reduce_scatter | solution.py:65
  7.9 0.9 copy-start.3
  11.2 77.7 %copy-start.4 = (bf16[48,16384]{1,0:T(8,128)(2,1)}, bf16[48,16384]{1,0:T(8,128)(2,1)S(1)}, u32[]{:S(2)}) copy-start(bf16[48,16384]{1,0:T(8,128)(2,1)S(1)} %reshape.25) | copy-start | bytes 4718596
  11.2 39.9 %collective-permute-start.2 = (bf16[48,16384]{1,0:T(8,128)(2,1)S(1)}, bf16[48,16384]{1,0:T(8,128)(2,1)}, u32[]{:S(2)}, u32[]{:S(2)}) collective-permute-start(bf16[48,16384]{1,0:T(8,128)(2,1)S(1)} %reshape.25), channel_id=1, source_target_pairs={{0,24},{8,0},{16,8},{24,16},{1,25},{9,1},{17,9},{25,17},{2,26},{10... | collective-permute-start | bytes 4718600 | tf_op jit(solution)/shard_map/ppermute | solution.py:12
  16.4 69.5 %collective-permute-start = (bf16[48,16384]{1,0:T(8,128)(2,1)S(1)}, bf16[48,16384]{1,0:T(8,128)(2,1)}, u32[]{:S(2)}, u32[]{:S(2)}) collective-permute-start(bf16[48,16384]{1,0:T(8,128)(2,1)S(1)} %reshape.25), channel_id=1, source_target_pairs={{0,8},{8,16},{16,24},{24,0},{1,9},{9,17},{17,25},{25,1},{2,10},{10... | collective-permute-start | bytes 4718600 | tf_op jit(solution)/shard_map/ppermute | solution.py:12
  51.2 103.0 %collective-permute-start.3 = (bf16[48,16384]{1,0:T(8,128)(2,1)}, bf16[48,16384]{1,0:T(8,128)(2,1)S(1)}, u32[]{:S(2)}, u32[]{:S(2)}) collective-permute-start(bf16[48,16384]{1,0:T(8,128)(2,1)} %collective-permute-done.2), channel_id=1, source_target_pairs={{0,24},{8,0},{16,8},{24,16},{1,25},{9,1},{17,9},{25,17},{2,26},{10... | collective-permute-start | bytes 4718600 | tf_op jit(solution)/shard_map/ppermute | solution.py:12
  85.9 66.2 %collective-permute-start.1 = (bf16[48,16384]{1,0:T(8,128)(2,1)}, bf16[48,16384]{1,0:T(8,128)(2,1)S(1)}, u32[]{:S(2)}, u32[]{:S(2)}) collective-permute-start(bf16[48,16384]{1,0:T(8,128)(2,1)} %collective-permute-done), channel_id=1, source_target_pairs={{0,8},{8,16},{16,24},{24,0},{1,9},{9,17},{17,25},{25,1},{2,10},{10... | collective-permute-start | bytes 4718600 | tf_op jit(solution)/shard_map/ppermute | solution.py:12
  154.3 1.7 copy-start
  219.4 4.5 %copy-start.1 = (bf16[96,16384]{1,0:T(8,128)(2,1)S(1)}, bf16[96,16384]{1,0:T(8,128)(2,1)}, u32[]{:S(2)}) copy-start(bf16[96,16384]{1,0:T(8,128)(2,1)} %get-tuple-element.200) | copy-start | bytes 9437188
Sparse Core Ops, SparseCore 0:
  222.1 25.0 reduce-scatter.1
where the time goes:
time: 257 us; the launch traced here: 256 us
  waiting for transfers between devices  145 us (56%)
  matrix products  41.9 us (16%)
  local copies, waits for them, and re-layouts  26.3 us (10%)
  between operations  13.5 us (5%)
  other arithmetic  11.8 us (5%)
  starting transfers between devices  11.1 us (4%)
  blocking collectives  5.74 us (2%)
    ppermute x4, waiting for transfers between devices, passed_along(): lax.ppermute(value, axis, [(i, (i + by) % count) for i in range(count)])  128 us
    dot_general x16, matrix products, add_block(): lax.dot_general(pair_rows, partner_cut, (((1,), (1,)), ((), ())), preferr...  41.9 us
    reduce_scatter x1, waiting for transfers between devices, body(): summed = lax.psum_scatter(tables, 'field', scatter_dimension=0, tiled=True)  16.8 us
    dynamic_slice x16, local copies, waits for them, and re-layouts, add_block(): third_cut = lax.dynamic_slice_in_dim(third_rows, offset, block_width, 1)  14.6 us
    ppermute x4, starting transfers between devices, passed_along(): lax.ppermute(value, axis, [(i, (i + by) % count) for i in range(count)])  11.1 us
    psum x1, blocking collectives, body(): lax.psum((row_totals(vector_rows), row_totals(third_rows), row_totals(par...  5.74 us
  transfers between devices with their start and end apart: 5, of which 4 were waited for; matrix products, arithmetic and copies ran while one was open for 2% of the time, Pallas kernels for 0%

commit v1 on v0

v1 whole, which is shorter than its diff:
```python
import functools

import jax
import jax.numpy as jnp
from jax import lax
from jax.experimental import pallas as pl
from jax.experimental.pallas import tpu as pltpu
from jax.sharding import PartitionSpec as P

MESH = pl.DeviceIdType.MESH
CHUNKS = 4
STEP = 512


def kernel(nv, nf, nr, fields, d_ref, o_ref, own, low, high, far, acc, outgoing, incoming,
           load_sem, ring_send, ring_recv, hop_send, hop_recv, table_send, table_recv):
    groups, _, half = own.shape
    vectors = groups * 8
    share = vectors // nf
    pair_rows = vectors * vectors
    plane_rows = pair_rows + vectors
    shared_far = far.shape[0] == 1
    width = half // CHUNKS
    members = nf * nr

    vec_at = lax.axis_index("vec")
    field_at = lax.axis_index("field")
    rep_at = lax.axis_index("rep")
    place = rep_at * nf + field_at
    above = {"vec": lax.rem(vec_at + 1, nv)}
    below = {"vec": lax.rem(vec_at + nv - 1, nv)}

    def member(offset):
        index = lax.rem(place + offset, members)
        return index, {"rep": index // nf, "field": lax.rem(index, nf)}

    load = pltpu.make_async_copy(
        d_ref.at[:, :, pl.ds(pl.multiple_of(rep_at * half, half), half)], own, load_sem
    )
    load.start()
    barrier = pltpu.get_barrier_semaphore()
    for target in (above, below):
        pl.semaphore_signal(barrier, inc=1, device_id=target, device_id_type=MESH)
    for offset in range(1, members):
        pl.semaphore_signal(barrier, inc=1, device_id=member(offset)[1], device_id_type=MESH)
    acc[...] = jnp.zeros_like(acc)
    load.wait()
    pl.semaphore_wait(barrier, members + 1)

    def own_copies(c):
        cut = pl.ds(c * width, width)
        return [
            pltpu.make_async_remote_copy(
                src_ref=own.at[:, :, cut], dst_ref=buffer.at[:, :, cut],
                send_sem=ring_send.at[way, c], recv_sem=ring_recv.at[way, c],
                device_id=target, device_id_type=MESH)
            for way, (buffer, target) in enumerate(((low, above), (high, below)))
        ]

    def hop_copies(c):
        copies = []
        for way, (buffer, target) in enumerate(((low, above), (high, below))):
            if shared_far:
                cut = pl.ds(c * width + way * (width // 2), width // 2)
                landing = far.at[0, :, :, cut]
            else:
                cut = pl.ds(c * width, width)
                landing = far.at[way, :, :, cut]
            copies.append(pltpu.make_async_remote_copy(
                src_ref=buffer.at[:, :, cut], dst_ref=landing,
                send_sem=hop_send.at[way, c], recv_sem=hop_recv.at[way, c],
                device_id=target, device_id_type=MESH))
        return copies

    def contract(c):
        def step(t, carry):
            cut = pl.ds(pl.multiple_of(c * width + t * STEP, STEP), STEP)

            def rows(block):
                return block.astype(jnp.float32).reshape(vectors, STEP)

            mine = rows(own[:, :, cut])
            thirds = [rows(low[:, :, cut]), rows(far[0, :, :, cut])]
            partners = [rows(high[:, :, cut]), thirds[1] if shared_far else rows(far[1, :, :, cut])]
            one = (lax.broadcasted_iota(jnp.int32, (8, STEP), 0) == 0).astype(jnp.float32)
            blank = jnp.zeros((8, STEP), jnp.float32)
            lines = []
            for third in thirds:
                for i in range(vectors):
                    lines.append(mine[i:i + 1] * third)
                lines.append(third)
            left = jnp.concatenate(lines + [mine, one], axis=0).astype(jnp.bfloat16)
            side = partners + [one, blank]
            right = jnp.concatenate(side + side, axis=0).astype(jnp.bfloat16)
            acc[...] += lax.dot_general(
                left, right, (((1,), (1,)), ((), ())), preferred_element_type=jnp.float32)
            return carry

        lax.fori_loop(0, width // STEP, step, 0)

    ring = [own_copies(c) for c in range(CHUNKS)]
    hops = [hop_copies(c) for c in range(CHUNKS)]

    def start(copies):
        for copy in copies:
            copy.start()

    def arrive(copies):
        for copy in copies:
            copy.wait_recv()

    for c in range(min(2, CHUNKS)):
        start(ring[c])
    for c in range(CHUNKS + 1):
        if c < CHUNKS:
            arrive(ring[c])
            start(hops[c])
            if c + 2 < CHUNKS:
                start(ring[c + 2])
        if c > 0:
            arrive(hops[c - 1])
            contract(c - 1)

    lanes = acc.shape[1]
    packed = share // 2 * vectors
    first_half = lax.broadcasted_iota(jnp.int32, (packed, lanes), 1) < lanes // 2
    for plane in range(nr):
        base = plane * plane_rows
        for s in range(nf):
            slot = plane * nf + s
            at = base + s * share * vectors
            outgoing[slot, 0:packed] = jnp.where(
                first_half, acc[at:at + packed], acc[at + packed:at + 2 * packed])
            outgoing[slot, packed:packed + vectors] = acc[base + pair_rows:base + plane_rows]
            tail = nr * plane_rows
            line = packed + vectors
            outgoing[slot, line:line + share] = acc[tail + s * share:tail + (s + 1) * share]
            outgoing[slot, line + share:line + share + 2] = acc[tail + vectors:tail + vectors + 2]

    shares = []
    for offset in range(1, members):
        index, target = member(offset)
        copy = pltpu.make_async_remote_copy(
            src_ref=outgoing.at[index], dst_ref=incoming.at[offset],
            send_sem=table_send.at[offset], recv_sem=table_recv.at[offset],
            device_id=target, device_id_type=MESH)
        copy.start()
        shares.append(copy)
    total = outgoing[place]
    for offset, copy in enumerate(shares, 1):
        copy.wait_recv()
        total = total + incoming[offset]

    count = share * vectors // 2
    cols = o_ref.shape[1]
    source = lax.broadcasted_iota(jnp.int32, (lanes, lanes), 0)
    landing = lax.broadcasted_iota(jnp.int32, (lanes, lanes), 1)
    spread = jnp.where(landing < cols, landing // 2, cols // 2)

    def spread_out(value, start_lane):
        return jnp.dot(value, (source == spread + start_lane).astype(jnp.float32),
                       precision=lax.Precision.HIGHEST, preferred_element_type=jnp.float32)

    early = spread_out(total, 0)
    late = spread_out(total[0:packed], lanes // 2)
    pick = lax.broadcasted_iota(jnp.int32, (1, lanes), 1) % 2 == 1
    third_rows = early[packed:packed + vectors]
    line = packed + vectors
    third_sum = third_rows[:, cols:cols + 1]
    partner_sum = early[line + share:line + share + 1]
    twice = 2.0 * fields

    def gain(value):
        return 1.0 - value / (3.0 * fields)

    partner_counts = jnp.where(pick, partner_sum, twice - partner_sum)
    third_partner = jnp.where(pick, third_rows, 2.0 * third_sum - third_rows)
    scale_partner = gain(partner_counts) * (4.5 / (8.0 * fields))
    scale_third = [gain(twice - third_sum), gain(third_sum)]
    for i in range(share):
        from_value = early if i < share // 2 else late
        at = (i % (share // 2)) * vectors
        table = from_value[at:at + vectors]
        both = table[:, cols:cols + 1]
        own_row = early[line + i:line + i + 1]
        own_sum = own_row[:, cols:cols + 1]
        own_partner = jnp.where(pick, own_row, 2.0 * own_sum - own_row)
        t11 = jnp.where(pick, table, 2.0 * both - table)
        t01 = 2.0 * third_partner - t11
        t10 = 2.0 * own_partner - t11
        t00 = 4.0 * partner_counts - 2.0 * own_partner - t01
        scale_own = [gain(twice - own_sum), gain(own_sum)]
        for a, c, value in ((0, 0, t00), (0, 1, t01), (1, 0, t10), (1, 1, t11)):
            result = value * scale_own[a] * scale_third[c] * scale_partner
            o_ref[pl.ds((i * 2 + a) * vectors * 2 + c, vectors, stride=2), :] = result[:, :cols]

    for copies in ring + hops + [shares]:
        for copy in copies:
            copy.wait_send()


def solution(mesh):
    nv, nf, nr = mesh.shape["vec"], mesh.shape["field"], mesh.shape["rep"]

    def body(dosage):
        vectors, slice_width = dosage.shape
        fields = slice_width * nf
        groups = vectors // 8
        half = slice_width // nr
        share = vectors // nf
        members = nf * nr
        rows = nr * (vectors * vectors + vectors) + vectors + 8
        chunk_rows = share // 2 * vectors + vectors + share + 2
        block = pltpu.VMEM((groups, 8, half), jnp.bfloat16)
        dma = pltpu.SemaphoreType.DMA
        out = pl.pallas_call(
            functools.partial(kernel, nv, nf, nr, float(fields)),
            out_shape=jax.ShapeDtypeStruct((share * 2 * vectors * 2, 4 * vectors), jnp.float32),
            in_specs=[pl.BlockSpec(memory_space=pl.ANY)],
            out_specs=pl.BlockSpec(memory_space=pltpu.VMEM),
            scratch_shapes=[
                block, block, block,
                pltpu.VMEM((1 if nv == 4 else 2, groups, 8, half), jnp.bfloat16),
                pltpu.VMEM((rows, 128), jnp.float32),
                pltpu.VMEM((members, chunk_rows, 128), jnp.float32),
                pltpu.VMEM((members, chunk_rows, 128), jnp.float32),
                dma(()), dma((2, CHUNKS)), dma((2, CHUNKS)), dma((2, CHUNKS)), dma((2, CHUNKS)),
                dma((members,)), dma((members,)),
            ],
            compiler_params=pltpu.CompilerParams(
                collective_id=0, has_side_effects=True, vmem_limit_bytes=60 * 1024 * 1024),
        )(dosage.reshape(groups, 8, slice_width))
        return out.reshape(1, share, 2, vectors, 2, 4 * vectors)

    return jax.shard_map(
        body,
        mesh=mesh,
        in_specs=(P("vec", "field"),),
        out_specs=P("rep", ("vec", "field"), None, None, None, None),
        check_vma=False,
    )
```

time: 257 us -> 43.9 us (0.17)
  waiting for transfers between devices: 145 us -> 0 us
  Pallas kernels: 0 us -> 42 us
  matrix products: 41.9 us -> 0 us
  local copies, waits for them, and re-layouts: 26.3 us -> 1.69 us
  between operations: 13.5 us -> 0.01 us
  other arithmetic: 11.8 us -> 0 us
  starting transfers between devices: 11.1 us -> 0 us
  blocking collectives: 5.74 us -> 0 us
    ppermute x4 -> x0, waiting for transfers between devices: 128 us -> none  [passed_along(): lax.ppermute(value, axis, [(i, (i + by) % count) for i in range(count)])]
    pallas_call x0 -> x1, Pallas kernels: none -> 42 us  [body(): pl.pallas_call(functools.partial(kernel, nv, nf, nr, float(fields)), out_...]
    dot_general x16 -> x0, matrix products: 41.9 us -> none  [add_block(): lax.dot_general(pair_rows, partner_cut, (((1,), (1,)), ((), ())), preferr...]
    reduce_scatter x1 -> x0, waiting for transfers between devices: 16.8 us -> none  [body(): summed = lax.psum_scatter(tables, 'field', scatter_dimension=0, tiled=True)]
    dynamic_slice x16 -> x0, local copies, waits for them, and re-layouts: 14.6 us -> none  [add_block(): third_cut = lax.dynamic_slice_in_dim(third_rows, offset, block_width, 1)]
    ppermute x4 -> x0, starting transfers between devices: 11.1 us -> none  [passed_along(): lax.ppermute(value, axis, [(i, (i + by) % count) for i in range(count)])]
    psum x1 -> x0, blocking collectives: 5.74 us -> none  [body(): lax.psum((row_totals(vector_rows), row_totals(third_rows), row_totals(par...]
    mul x17 -> x0, other arithmetic: 4.97 us -> none  [the longest x16 4.95 us: add_block(): first_cut[:, None, :] * third_cut[None, :, :]]
  transfers between devices with their start and end apart: 5 -> 0, of which waited for: 4 -> 0; matrix products, arithmetic and copies ran while one was open for 2% -> 0% of each run, Pallas kernels for 0% -> 0%
where the time goes in v1:
time: 43.9 us; the launch traced here: 43.7 us
  Pallas kernels  42 us (96%)
  local copies, waits for them, and re-layouts  1.69 us (4%)
    pallas_call x1, Pallas kernels, body(): pl.pallas_call(functools.partial(kernel, nv, nf, nr, float(fields)), out_...  42 us
    unnamed x1, local copies, waits for them, and re-layouts  1.69 us

profile of v1, /device:TPU:0, one launch (start us, length us, event | category | flops | bytes accessed | tf_op | source)
XLA Modules:
  0.0 43.7 jit_solution(2395003692017875517)
XLA Ops:
  0.0 42.0 %shard_map.17 = f32[576,96]{1,0:T(8,128)} custom-call(bf16[3,8,16384]{2,1,0:T(8,128)(2,1)} %bitcast.3), custom_call_target="tpu_custom_call" | custom-call | tf_op jit(solution)/shard_map/pallas_call | solution.py:216
  42.0 1.7 %copy.3 = f32[1,6,2,24,2,96]{5,4,3,2,1,0:T(2,128)} copy(f32[1,6,2,24,2,96]{5,4,3,2,1,0:T(2,128)} %bitcast.2) | data formatting | bytes 442368

commit v2 on v1

v2 whole, which is shorter than its diff:
```python
import functools

import jax
import jax.numpy as jnp
from jax import lax
from jax.experimental import pallas as pl
from jax.experimental.pallas import tpu as pltpu
from jax.sharding import PartitionSpec as P

MESH = pl.DeviceIdType.MESH
CHUNKS = 4
STEP = 512


def triples(mine, thirds, partners):
    vectors, width = mine.shape
    one = (lax.broadcasted_iota(jnp.int32, (8, width), 0) == 0).astype(jnp.float32)
    blank = jnp.zeros((8, width), jnp.float32)
    lines = []
    for third in thirds:
        for i in range(vectors):
            lines.append(mine[i:i + 1] * third)
        lines.append(third)
    left = jnp.concatenate(lines + [mine, one], axis=0).astype(jnp.bfloat16)
    side = partners + [one, blank]
    right = jnp.concatenate(side + side, axis=0).astype(jnp.bfloat16)
    return lax.dot_general(left, right, (((1,), (1,)), ((), ())), preferred_element_type=jnp.float32)


def pack(chunk, acc, plane, s, nr, share, vectors):
    lanes = acc.shape[1]
    pair_rows = vectors * vectors
    plane_rows = pair_rows + vectors
    packed = share // 2 * vectors
    first_half = lax.broadcasted_iota(jnp.int32, (packed, lanes), 1) < lanes // 2
    base = plane * plane_rows
    at = base + s * share * vectors
    tail = nr * plane_rows
    line = packed + vectors
    chunk[0:packed] = jnp.where(first_half, acc[at:at + packed], acc[at + packed:at + 2 * packed])
    chunk[packed:line] = acc[base + pair_rows:base + plane_rows]
    chunk[line:line + share] = acc[tail + s * share:tail + (s + 1) * share]
    chunk[line + share:line + share + 2] = acc[tail + vectors:tail + vectors + 2]


def finish(total, o_ref, fields, share, vectors):
    lanes = total.shape[1]
    packed = share // 2 * vectors
    cols = o_ref.shape[1]
    source = lax.broadcasted_iota(jnp.int32, (lanes, lanes), 0)
    landing = lax.broadcasted_iota(jnp.int32, (lanes, lanes), 1)
    spread = jnp.where(landing < cols, landing // 2, cols // 2)

    def spread_out(value, start_lane):
        return jnp.dot(value, (source == spread + start_lane).astype(jnp.float32),
                       precision=lax.Precision.HIGHEST, preferred_element_type=jnp.float32)

    early = spread_out(total, 0)
    late = spread_out(total[0:packed], lanes // 2)
    pick = lax.broadcasted_iota(jnp.int32, (1, lanes), 1) % 2 == 1
    third_rows = early[packed:packed + vectors]
    line = packed + vectors
    third_sum = third_rows[:, cols:cols + 1]
    partner_sum = early[line + share:line + share + 1]
    twice = 2.0 * fields

    def gain(value):
        return 1.0 - value / (3.0 * fields)

    partner_counts = jnp.where(pick, partner_sum, twice - partner_sum)
    third_partner = jnp.where(pick, third_rows, 2.0 * third_sum - third_rows)
    scale_partner = gain(partner_counts) * (4.5 / (8.0 * fields))
    scale_third = [gain(twice - third_sum), gain(third_sum)]
    for i in range(share):
        from_value = early if i < share // 2 else late
        at = (i % (share // 2)) * vectors
        table = from_value[at:at + vectors]
        both = table[:, cols:cols + 1]
        own_row = early[line + i:line + i + 1]
        own_sum = own_row[:, cols:cols + 1]
        own_partner = jnp.where(pick, own_row, 2.0 * own_sum - own_row)
        t11 = jnp.where(pick, table, 2.0 * both - table)
        t01 = 2.0 * third_partner - t11
        t10 = 2.0 * own_partner - t11
        t00 = 4.0 * partner_counts - 2.0 * own_partner - t01
        scale_own = [gain(twice - own_sum), gain(own_sum)]
        for a, c, value in ((0, 0, t00), (0, 1, t01), (1, 0, t10), (1, 1, t11)):
            result = value * scale_own[a] * scale_third[c] * scale_partner
            o_ref[pl.ds((i * 2 + a) * vectors * 2 + c, vectors, stride=2), :] = result[:, :cols]


def kernel(nv, nf, nr, fields, d_ref, o_ref, own, low, high, far, acc, outgoing, incoming,
           load_sem, ring_send, ring_recv, hop_send, hop_recv, table_send, table_recv):
    groups, _, half = own.shape
    vectors = groups * 8
    share = vectors // nf
    pair_rows = vectors * vectors
    plane_rows = pair_rows + vectors
    shared_far = far.shape[0] == 1
    width = half // CHUNKS
    members = nf * nr

    vec_at = lax.axis_index("vec")
    field_at = lax.axis_index("field")
    rep_at = lax.axis_index("rep")
    place = rep_at * nf + field_at
    above = {"vec": lax.rem(vec_at + 1, nv)}
    below = {"vec": lax.rem(vec_at + nv - 1, nv)}

    def member(offset):
        index = lax.rem(place + offset, members)
        return index, {"rep": index // nf, "field": lax.rem(index, nf)}

    load = pltpu.make_async_copy(
        d_ref.at[:, :, pl.ds(pl.multiple_of(rep_at * half, half), half)], own, load_sem
    )
    load.start()
    barrier = pltpu.get_barrier_semaphore()
    for target in (above, below):
        pl.semaphore_signal(barrier, inc=1, device_id=target, device_id_type=MESH)
    for offset in range(1, members):
        pl.semaphore_signal(barrier, inc=1, device_id=member(offset)[1], device_id_type=MESH)
    acc[...] = jnp.zeros_like(acc)
    load.wait()
    pl.semaphore_wait(barrier, members + 1)

    def own_copies(c):
        cut = pl.ds(c * width, width)
        return [
            pltpu.make_async_remote_copy(
                src_ref=own.at[:, :, cut], dst_ref=buffer.at[:, :, cut],
                send_sem=ring_send.at[way, c], recv_sem=ring_recv.at[way, c],
                device_id=target, device_id_type=MESH)
            for way, (buffer, target) in enumerate(((low, above), (high, below)))
        ]

    def hop_copies(c):
        copies = []
        for way, (buffer, target) in enumerate(((low, above), (high, below))):
            if shared_far:
                cut = pl.ds(c * width + way * (width // 2), width // 2)
                landing = far.at[0, :, :, cut]
            else:
                cut = pl.ds(c * width, width)
                landing = far.at[way, :, :, cut]
            copies.append(pltpu.make_async_remote_copy(
                src_ref=buffer.at[:, :, cut], dst_ref=landing,
                send_sem=hop_send.at[way, c], recv_sem=hop_recv.at[way, c],
                device_id=target, device_id_type=MESH))
        return copies

    def contract(c):
        def step(t, carry):
            cut = pl.ds(pl.multiple_of(c * width + t * STEP, STEP), STEP)

            def rows(block):
                return block.astype(jnp.float32).reshape(vectors, STEP)

            mine = rows(own[:, :, cut])
            thirds = [rows(low[:, :, cut]), rows(far[0, :, :, cut])]
            partners = [rows(high[:, :, cut]), thirds[1] if shared_far else rows(far[1, :, :, cut])]
            acc[...] += triples(mine, thirds, partners)
            return carry

        lax.fori_loop(0, width // STEP, step, 0)

    ring = [own_copies(c) for c in range(CHUNKS)]
    hops = [hop_copies(c) for c in range(CHUNKS)]

    def start(copies):
        for copy in copies:
            copy.start()

    def arrive(copies):
        for copy in copies:
            copy.wait_recv()

    for c in range(min(2, CHUNKS)):
        start(ring[c])
    for c in range(CHUNKS + 1):
        if c < CHUNKS:
            arrive(ring[c])
            start(hops[c])
            if c + 2 < CHUNKS:
                start(ring[c + 2])
        if c > 0:
            arrive(hops[c - 1])
            contract(c - 1)

    for plane in range(nr):
        for s in range(nf):
            pack(outgoing.at[plane * nf + s], acc, plane, s, nr, share, vectors)

    shares = []
    for offset in range(1, members):
        index, target = member(offset)
        copy = pltpu.make_async_remote_copy(
            src_ref=outgoing.at[index], dst_ref=incoming.at[offset],
            send_sem=table_send.at[offset], recv_sem=table_recv.at[offset],
            device_id=target, device_id_type=MESH)
        copy.start()
        shares.append(copy)
    total = outgoing[place]
    for offset, copy in enumerate(shares, 1):
        copy.wait_recv()
        total = total + incoming[offset]

    finish(total, o_ref, fields, share, vectors)
    for copies in ring + hops + [shares]:
        for copy in copies:
            copy.wait_send()


def quad_kernel(nf, nr, fields, d_ref, o_ref, blocks, ship, acc, outgoing, mates, summed, incoming,
                handoff, handed, load_sem, ring_send, ring_recv, hop_send,
                mate_sem, table_send, table_recv, hand_sem):
    _, groups, _, quarter = blocks.shape
    vectors = groups * 8
    share = vectors // nf
    columns = nf // 2
    seats = nr * columns
    width = quarter // CHUNKS

    z = lax.axis_index("vec")
    field_at = lax.axis_index("field")
    rep_at = lax.axis_index("rep")
    group = z // 2
    mate = z + 1 - 2 * lax.rem(z, 2)
    across = 2 - group
    across_end = 3 * (1 - group)
    middle = z == 1 + group
    core = lax.rem(field_at, 2)
    seat = rep_at * columns + field_at // 2
    partner = {"field": field_at + 1 - 2 * core}

    def seat_of(offset):
        index = lax.rem(seat + offset, seats)
        return index, {"rep": index // columns, "field": lax.rem(index, columns) * 2 + core}

    start_column = rep_at * 2 * quarter

    def part(g):
        return d_ref.at[:, :, pl.ds(pl.multiple_of(start_column + g * quarter, quarter), quarter)]

    loads = [pltpu.make_async_copy(part(1 - group), ship, load_sem.at[0]),
             pltpu.make_async_copy(part(group), blocks.at[z], load_sem.at[1])]
    for load in loads:
        load.start()
    barrier = pltpu.get_barrier_semaphore()
    for offset in range(1, 4):
        pl.semaphore_signal(barrier, inc=1, device_id={"vec": lax.rem(z + offset, 4)}, device_id_type=MESH)
    pl.semaphore_signal(barrier, inc=1, device_id=partner, device_id_type=MESH)
    for offset in range(1, seats):
        pl.semaphore_signal(barrier, inc=1, device_id=seat_of(offset)[1], device_id_type=MESH)
    acc[...] = jnp.zeros_like(acc)
    for load in loads:
        load.wait()
    pl.semaphore_wait(barrier, 3 + seats)

    def sent(source, block, c, send_sem, target):
        cut = pl.ds(c * width, width)
        return pltpu.make_async_remote_copy(
            src_ref=source.at[:, :, cut], dst_ref=blocks.at[block, :, :, cut],
            send_sem=send_sem, recv_sem=ring_recv.at[block, c],
            device_id={"vec": target}, device_id_type=MESH)

    firsts = []
    for c in range(CHUNKS):
        firsts.append(sent(ship, z, c, ring_send.at[0, c], across))
        firsts.append(sent(blocks.at[z], z, c, ring_send.at[1, c], mate))
    for copy in firsts:
        copy.start()

    def hop(k, c):
        block = (across, across_end)[k]
        return sent(blocks.at[block], block, c, hop_send.at[k, c], mate)

    def arrive(c, forward):
        for k in range(2):
            hop(k, c).wait_recv()
            if forward:
                hop(k, c).start()
        sent(blocks.at[mate], mate, c, hop_send.at[0, c], mate).wait_recv()

    def contract(c):
        def step(t, carry):
            cut = pl.ds(pl.multiple_of(c * width + t * STEP, STEP), STEP)
            mine, high, far, low = [
                blocks[lax.rem(z + k, 4), :, :, cut].astype(jnp.float32).reshape(vectors, STEP)
                for k in range(4)]
            acc[0] += triples(mine, [low, far], [high, far])
            acc[1] += triples(far, [high, mine], [low, mine])
            return carry

        lax.fori_loop(0, width // STEP, step, 0)

    pl.when(middle)(lambda: arrive(0, True))
    for c in range(CHUNKS):
        if c + 1 < CHUNKS:
            pl.when(middle)(functools.partial(arrive, c + 1, True))
        pl.when(jnp.logical_not(middle))(functools.partial(arrive, c, False))
        contract(c)

    for kind in range(2):
        for plane in range(nr):
            for s in range(nf):
                pack(outgoing.at[s % 2, plane * columns + s // 2, kind], acc.at[kind],
                     plane, s, nr, share, vectors)
    swap = pltpu.make_async_remote_copy(
        src_ref=outgoing.at[1 - core], dst_ref=mates, send_sem=mate_sem.at[0], recv_sem=mate_sem.at[1],
        device_id=partner, device_id_type=MESH)
    swap.start()
    swap.wait_recv()
    summed[...] = outgoing[core] + mates[...]
    shares = []
    for offset in range(1, seats):
        index, target = seat_of(offset)
        copy = pltpu.make_async_remote_copy(
            src_ref=summed.at[index], dst_ref=incoming.at[offset],
            send_sem=table_send.at[offset], recv_sem=table_recv.at[offset],
            device_id=target, device_id_type=MESH)
        copy.start()
        shares.append(copy)
    both = summed[seat]
    for offset, copy in enumerate(shares, 1):
        copy.wait_recv()
        both = both + incoming[offset]
    handoff[...] = both[1]
    hand = pltpu.make_async_remote_copy(
        src_ref=handoff, dst_ref=handed, send_sem=hand_sem.at[0], recv_sem=hand_sem.at[1],
        device_id={"vec": lax.rem(z + 2, 4)}, device_id_type=MESH)
    hand.start()
    hand.wait_recv()
    finish(both[0] + handed[...], o_ref, fields, share, vectors)

    for copy in firsts + shares + [swap, hand]:
        copy.wait_send()

    def drain():
        for c in range(CHUNKS):
            for k in range(2):
                hop(k, c).wait_send()

    pl.when(middle)(drain)


def quad_scratch(groups, quarter, rows, chunk_rows, seats):
    dma = pltpu.SemaphoreType.DMA
    return [
        pltpu.VMEM((4, groups, 8, quarter), jnp.bfloat16),
        pltpu.VMEM((groups, 8, quarter), jnp.bfloat16),
        pltpu.VMEM((2, rows, 128), jnp.float32),
        pltpu.VMEM((2, seats, 2, chunk_rows, 128), jnp.float32),
        pltpu.VMEM((seats, 2, chunk_rows, 128), jnp.float32),
        pltpu.VMEM((seats, 2, chunk_rows, 128), jnp.float32),
        pltpu.VMEM((seats, 2, chunk_rows, 128), jnp.float32),
        pltpu.VMEM((chunk_rows, 128), jnp.float32),
        pltpu.VMEM((chunk_rows, 128), jnp.float32),
        dma((2,)), dma((2, CHUNKS)), dma((4, CHUNKS)), dma((2, CHUNKS)),
        dma((2,)), dma((seats,)), dma((seats,)), dma((2,)),
    ]


def solution(mesh):
    nv, nf, nr = mesh.shape["vec"], mesh.shape["field"], mesh.shape["rep"]

    def body(dosage):
        vectors, slice_width = dosage.shape
        fields = slice_width * nf
        groups = vectors // 8
        half = slice_width // nr
        share = vectors // nf
        members = nf * nr
        rows = nr * (vectors * vectors + vectors) + vectors + 8
        chunk_rows = share // 2 * vectors + vectors + share + 2
        block = pltpu.VMEM((groups, 8, half), jnp.bfloat16)
        dma = pltpu.SemaphoreType.DMA
        if nv == 4:
            run = functools.partial(quad_kernel, nf, nr, float(fields))
            scratch = quad_scratch(groups, half // 2, rows, chunk_rows, members // 2)
        else:
            run = functools.partial(kernel, nv, nf, nr, float(fields))
            scratch = [
                block, block, block,
                pltpu.VMEM((1 if nv == 4 else 2, groups, 8, half), jnp.bfloat16),
                pltpu.VMEM((rows, 128), jnp.float32),
                pltpu.VMEM((members, chunk_rows, 128), jnp.float32),
                pltpu.VMEM((members, chunk_rows, 128), jnp.float32),
                dma(()), dma((2, CHUNKS)), dma((2, CHUNKS)), dma((2, CHUNKS)), dma((2, CHUNKS)),
                dma((members,)), dma((members,)),
            ]
        out = pl.pallas_call(
            run,
            out_shape=jax.ShapeDtypeStruct((share * 2 * vectors * 2, 4 * vectors), jnp.float32),
            in_specs=[pl.BlockSpec(memory_space=pl.ANY)],
            out_specs=pl.BlockSpec(memory_space=pltpu.VMEM),
            scratch_shapes=scratch,
            compiler_params=pltpu.CompilerParams(
                collective_id=0, has_side_effects=True, vmem_limit_bytes=60 * 1024 * 1024),
        )(dosage.reshape(groups, 8, slice_width))
        return out.reshape(1, share, 2, vectors, 2, 4 * vectors)

    return jax.shard_map(
        body,
        mesh=mesh,
        in_specs=(P("vec", "field"),),
        out_specs=P("rep", ("vec", "field"), None, None, None, None),
        check_vma=False,
    )
```

time: 43.9 us -> 33.4 us (0.76)
  the two profiles are of different devices: /device:TPU:0 before, /device:TPU:13 now
where the time goes in v2:
time: 33.4 us; the launch traced here: 33.3 us
  Pallas kernels  31.6 us (95%)
  local copies, waits for them, and re-layouts  1.69 us (5%)
    pallas_call x1, Pallas kernels, body(): pl.pallas_call(run, out_shape=jax.ShapeDtypeStruct((share * 2 * vectors *...  31.6 us
    unnamed x1, local copies, waits for them, and re-layouts  1.69 us

profile of v2, /device:TPU:13, one launch (start us, length us, event | category | flops | bytes accessed | tf_op | source)
XLA Modules:
  0.0 33.3 jit_solution(3104421389608644073)
XLA Ops:
  0.0 31.6 %shard_map.17 = f32[576,96]{1,0:T(8,128)} custom-call(bf16[3,8,16384]{2,1,0:T(8,128)(2,1)} %bitcast.3), custom_call_target="tpu_custom_call" | custom-call | tf_op jit(solution)/shard_map/pallas_call | solution.py:392
  31.6 1.7 %copy.3 = f32[1,6,2,24,2,96]{5,4,3,2,1,0:T(2,128)} copy(f32[1,6,2,24,2,96]{5,4,3,2,1,0:T(2,128)} %bitcast.2) | data formatting | bytes 442368

commit v3 on v2

--- a/solution.py
+++ b/solution.py
@@ -282,14 +282,16 @@
                 hop(k, c).start()
         sent(blocks.at[mate], mate, c, hop_send.at[0, c], mate).wait_recv()
 
-    def contract(c):
+    def contract(c, kinds):
         def step(t, carry):
             cut = pl.ds(pl.multiple_of(c * width + t * STEP, STEP), STEP)
             mine, high, far, low = [
                 blocks[lax.rem(z + k, 4), :, :, cut].astype(jnp.float32).reshape(vectors, STEP)
                 for k in range(4)]
-            acc[0] += triples(mine, [low, far], [high, far])
-            acc[1] += triples(far, [high, mine], [low, mine])
+            if 0 in kinds:
+                acc[0] += triples(mine, [low, far], [high, far])
+            if 1 in kinds:
+                acc[1] += triples(far, [high, mine], [low, mine])
             return carry
 
         lax.fori_loop(0, width // STEP, step, 0)
@@ -299,41 +301,53 @@
         if c + 1 < CHUNKS:
             pl.when(middle)(functools.partial(arrive, c + 1, True))
         pl.when(jnp.logical_not(middle))(functools.partial(arrive, c, False))
-        contract(c)
-
-    for kind in range(2):
+        if c + 1 < CHUNKS:
+            contract(c, (0, 1))
+
+    swaps = {}
+    for kind in (1, 0):
+        contract(CHUNKS - 1, (kind,))
         for plane in range(nr):
             for s in range(nf):
-                pack(outgoing.at[s % 2, plane * columns + s // 2, kind], acc.at[kind],
+                pack(outgoing.at[s % 2, kind, plane * columns + s // 2], acc.at[kind],
                      plane, s, nr, share, vectors)
-    swap = pltpu.make_async_remote_copy(
-        src_ref=outgoing.at[1 - core], dst_ref=mates, send_sem=mate_sem.at[0], recv_sem=mate_sem.at[1],
-        device_id=partner, device_id_type=MESH)
-    swap.start()
-    swap.wait_recv()
-    summed[...] = outgoing[core] + mates[...]
-    shares = []
-    for offset in range(1, seats):
-        index, target = seat_of(offset)
-        copy = pltpu.make_async_remote_copy(
-            src_ref=summed.at[index], dst_ref=incoming.at[offset],
-            send_sem=table_send.at[offset], recv_sem=table_recv.at[offset],
-            device_id=target, device_id_type=MESH)
-        copy.start()
-        shares.append(copy)
-    both = summed[seat]
-    for offset, copy in enumerate(shares, 1):
-        copy.wait_recv()
-        both = both + incoming[offset]
-    handoff[...] = both[1]
+        swaps[kind] = pltpu.make_async_remote_copy(
+            src_ref=outgoing.at[1 - core, kind], dst_ref=mates.at[kind],
+            send_sem=mate_sem.at[0, kind], recv_sem=mate_sem.at[1, kind],
+            device_id=partner, device_id_type=MESH)
+        swaps[kind].start()
+
+    shares = {}
+    for kind in (1, 0):
+        swaps[kind].wait_recv()
+        summed[kind] = outgoing[core, kind] + mates[kind]
+        shares[kind] = []
+        for offset in range(1, seats):
+            index, target = seat_of(offset)
+            copy = pltpu.make_async_remote_copy(
+                src_ref=summed.at[kind, index], dst_ref=incoming.at[kind, offset],
+                send_sem=table_send.at[kind, offset], recv_sem=table_recv.at[kind, offset],
+                device_id=target, device_id_type=MESH)
+            copy.start()
+            shares[kind].append(copy)
+
+    def gathered(kind):
+        total = summed[kind, seat]
+        for offset, copy in enumerate(shares[kind], 1):
+            copy.wait_recv()
+            total = total + incoming[kind, offset]
+        return total
+
+    handoff[...] = gathered(1)
     hand = pltpu.make_async_remote_copy(
         src_ref=handoff, dst_ref=handed, send_sem=hand_sem.at[0], recv_sem=hand_sem.at[1],
         device_id={"vec": lax.rem(z + 2, 4)}, device_id_type=MESH)
     hand.start()
+    kept = gathered(0)
     hand.wait_recv()
-    finish(both[0] + handed[...], o_ref, fields, share, vectors)
-
-    for copy in firsts + shares + [swap, hand]:
+    finish(kept + handed[...], o_ref, fields, share, vectors)
+
+    for copy in firsts + shares[0] + shares[1] + [swaps[0], swaps[1], hand]:
         copy.wait_send()
 
     def drain():
@@ -350,14 +364,14 @@
         pltpu.VMEM((4, groups, 8, quarter), jnp.bfloat16),
         pltpu.VMEM((groups, 8, quarter), jnp.bfloat16),
         pltpu.VMEM((2, rows, 128), jnp.float32),
-        pltpu.VMEM((2, seats, 2, chunk_rows, 128), jnp.float32),
-        pltpu.VMEM((seats, 2, chunk_rows, 128), jnp.float32),
-        pltpu.VMEM((seats, 2, chunk_rows, 128), jnp.float32),
-        pltpu.VMEM((seats, 2, chunk_rows, 128), jnp.float32),
+        pltpu.VMEM((2, 2, seats, chunk_rows, 128), jnp.float32),
+        pltpu.VMEM((2, seats, chunk_rows, 128), jnp.float32),
+        pltpu.VMEM((2, seats, chunk_rows, 128), jnp.float32),
+        pltpu.VMEM((2, seats, chunk_rows, 128), jnp.float32),
         pltpu.VMEM((chunk_rows, 128), jnp.float32),
         pltpu.VMEM((chunk_rows, 128), jnp.float32),
         dma((2,)), dma((2, CHUNKS)), dma((4, CHUNKS)), dma((2, CHUNKS)),
-        dma((2,)), dma((seats,)), dma((seats,)), dma((2,)),
+        dma((2, 2)), dma((2, seats)), dma((2, seats)), dma((2,)),
     ]
 
 

time: 33.4 us -> 32.3 us (0.967)
  the two profiles are of different devices: /device:TPU:13 before, /device:TPU:0 now
where the time goes in v3:
time: 32.3 us; the launch traced here: 32.2 us
  Pallas kernels  30.5 us (94%)
  local copies, waits for them, and re-layouts  1.69 us (5%)
    pallas_call x1, Pallas kernels, body(): pl.pallas_call(run, out_shape=jax.ShapeDtypeStruct((share * 2 * vectors *...  30.5 us
    unnamed x1, local copies, waits for them, and re-layouts  1.69 us

profile of v3, /device:TPU:0, one launch (start us, length us, event | category | flops | bytes accessed | tf_op | source)
XLA Modules:
  0.0 32.2 jit_solution(17665398502721898458)
XLA Ops:
  0.0 30.5 %shard_map.17 = f32[576,96]{1,0:T(8,128)} custom-call(bf16[3,8,16384]{2,1,0:T(8,128)(2,1)} %bitcast.3), custom_call_target="tpu_custom_call" | custom-call | tf_op jit(solution)/shard_map/pallas_call | solution.py:406
  30.5 1.7 %copy.3 = f32[1,6,2,24,2,96]{5,4,3,2,1,0:T(2,128)} copy(f32[1,6,2,24,2,96]{5,4,3,2,1,0:T(2,128)} %bitcast.2) | data formatting | bytes 442368

commit v4 on v3

--- a/solution.py
+++ b/solution.py
@@ -36,9 +36,12 @@
     base = plane * plane_rows
     at = base + s * share * vectors
     tail = nr * plane_rows
-    line = packed + vectors
+    half = vectors // 2
+    line = packed + half
+    thirds = base + pair_rows
     chunk[0:packed] = jnp.where(first_half, acc[at:at + packed], acc[at + packed:at + 2 * packed])
-    chunk[packed:line] = acc[base + pair_rows:base + plane_rows]
+    chunk[packed:line] = jnp.where(
+        first_half[0:half], acc[thirds:thirds + half], acc[thirds + half:thirds + vectors])
     chunk[line:line + share] = acc[tail + s * share:tail + (s + 1) * share]
     chunk[line + share:line + share + 2] = acc[tail + vectors:tail + vectors + 2]
 
@@ -46,6 +49,7 @@
 def finish(total, o_ref, fields, share, vectors):
     lanes = total.shape[1]
     packed = share // 2 * vectors
+    line = packed + vectors // 2
     cols = o_ref.shape[1]
     source = lax.broadcasted_iota(jnp.int32, (lanes, lanes), 0)
     landing = lax.broadcasted_iota(jnp.int32, (lanes, lanes), 1)
@@ -56,10 +60,9 @@
                        precision=lax.Precision.HIGHEST, preferred_element_type=jnp.float32)
 
     early = spread_out(total, 0)
-    late = spread_out(total[0:packed], lanes // 2)
+    late = spread_out(total[0:line], lanes // 2)
     pick = lax.broadcasted_iota(jnp.int32, (1, lanes), 1) % 2 == 1
-    third_rows = early[packed:packed + vectors]
-    line = packed + vectors
+    third_rows = jnp.concatenate([early[packed:line], late[packed:line]], axis=0)
     third_sum = third_rows[:, cols:cols + 1]
     partner_sum = early[line + share:line + share + 1]
     twice = 2.0 * fields
@@ -89,6 +92,10 @@
             o_ref[pl.ds((i * 2 + a) * vectors * 2 + c, vectors, stride=2), :] = result[:, :cols]
 
 
+def finish_kernel(fields, share, vectors, total_ref, o_ref):
+    finish(total_ref[...], o_ref, fields, share, vectors)
+
+
 def kernel(nv, nf, nr, fields, d_ref, o_ref, own, low, high, far, acc, outgoing, incoming,
            load_sem, ring_send, ring_recv, hop_send, hop_recv, table_send, table_recv):
     groups, _, half = own.shape
@@ -205,7 +212,7 @@
         copy.wait_recv()
         total = total + incoming[offset]
 
-    finish(total, o_ref, fields, share, vectors)
+    o_ref[...] = total
     for copies in ring + hops + [shares]:
         for copy in copies:
             copy.wait_send()
@@ -345,7 +352,7 @@
     hand.start()
     kept = gathered(0)
     hand.wait_recv()
-    finish(kept + handed[...], o_ref, fields, share, vectors)
+    o_ref[...] = kept + handed[...]
 
     for copy in firsts + shares[0] + shares[1] + [swaps[0], swaps[1], hand]:
         copy.wait_send()
@@ -386,7 +393,7 @@
         share = vectors // nf
         members = nf * nr
         rows = nr * (vectors * vectors + vectors) + vectors + 8
-        chunk_rows = share // 2 * vectors + vectors + share + 2
+        chunk_rows = share // 2 * vectors + vectors // 2 + share + 2
         block = pltpu.VMEM((groups, 8, half), jnp.bfloat16)
         dma = pltpu.SemaphoreType.DMA
         if nv == 4:
@@ -403,15 +410,19 @@
                 dma(()), dma((2, CHUNKS)), dma((2, CHUNKS)), dma((2, CHUNKS)), dma((2, CHUNKS)),
                 dma((members,)), dma((members,)),
             ]
-        out = pl.pallas_call(
+        total = pl.pallas_call(
             run,
-            out_shape=jax.ShapeDtypeStruct((share * 2 * vectors * 2, 4 * vectors), jnp.float32),
+            out_shape=jax.ShapeDtypeStruct((chunk_rows, 128), jnp.float32),
             in_specs=[pl.BlockSpec(memory_space=pl.ANY)],
             out_specs=pl.BlockSpec(memory_space=pltpu.VMEM),
             scratch_shapes=scratch,
             compiler_params=pltpu.CompilerParams(
                 collective_id=0, has_side_effects=True, vmem_limit_bytes=60 * 1024 * 1024),
         )(dosage.reshape(groups, 8, slice_width))
+        out = pl.pallas_call(
+            functools.partial(finish_kernel, float(fields), share, vectors),
+            out_shape=jax.ShapeDtypeStruct((share * 2 * vectors * 2, 4 * vectors), jnp.float32),
+        )(total)
         return out.reshape(1, share, 2, vectors, 2, 4 * vectors)
 
     return jax.shard_map(

time: 32.3 us -> 31.6 us (0.978)
  local copies, waits for them, and re-layouts: 1.69 us -> 0 us
  Pallas kernels: 30.5 us -> 31.4 us
    unnamed x1 -> x0, local copies, waits for them, and re-layouts: 1.69 us -> none
    pallas_call x1 -> x2, Pallas kernels: 30.5 us -> 31.4 us  [the longest x1 29.5 us: body(): pl.pallas_call(run, out_shape=jax.ShapeDtypeStruct((chunk_rows, 128), jnp...]
where the time goes in v4:
time: 31.6 us; the launch traced here: 31.4 us
  Pallas kernels  31.4 us (99%)
    pallas_call x1, Pallas kernels, body(): pl.pallas_call(run, out_shape=jax.ShapeDtypeStruct((chunk_rows, 128), jnp...  29.5 us
    pallas_call x1, Pallas kernels, body(): pl.pallas_call(functools.partial(finish_kernel, float(fields), share, vec...  1.91 us

profile of v4, /device:TPU:0, one launch (start us, length us, event | category | flops | bytes accessed | tf_op | source)
XLA Modules:
  0.0 31.4 jit_solution(1722823860828168910)
XLA Ops:
  0.0 29.5 %shard_map.17.total_ref = f32[92,128]{1,0:T(8,128)} custom-call(bf16[3,8,16384]{2,1,0:T(8,128)(2,1)} %bitcast.2), custom_call_target="tpu_custom_call" | custom-call | tf_op jit(solution)/shard_map/pallas_call | solution.py:413
  29.5 1.9 %shard_map.18 = f32[576,96]{1,0:T(8,128)} custom-call(f32[92,128]{1,0:T(8,128)} %shard_map.17.total_ref), custom_call_target="tpu_custom_call" | custom-call | tf_op jit(solution)/shard_map/pallas_call | solution.py:422
